TPU v7x, 32 devices: a whole 2x2x4 slice. The times are simulated.
32 devices in a mesh: section: 4 (over z), shard: 8 (over y, x, core).
Axes of the slice: x: 2, y: 2, z: 4, core: 2. Of those that a mesh axis runs over, the one named last changes fastest.
Arguments:
- grad_parts: bfloat16 [4, 8, 256, 8192], P('section', 'shard'), may hold values from -6 to 6
- params: bfloat16 [4, 256, 8192], P('section', 'shard'), may hold values from -6 to 6
- moment_first: float32 [4, 256, 8192], P('section', 'shard'), may hold values from -6 to 6
- moment_second: float32 [4, 256, 8192], P('section', 'shard'), may hold values from 0.5 to 50
- block_layer: int32 [4, 32], P('section', 'shard'), may hold values from 0 to 7, as said below
- block_valid: int32 [4, 32], P('section', 'shard'), may hold values from 0 to 1
- decay: float32 [8], replicated, may hold values from 0.05 to 1
Outputs:
- new_params: bfloat16 [4, 256, 8192], P('section', 'shard')
- new_first: float32 [4, 256, 8192], P('section', 'shard')
- new_second: float32 [4, 256, 8192], P('section', 'shard')
- ratios: float32 [8], replicated
Inputs may be any that keep to these rules, and one draw needn't show every extreme that they name: `block_layer`: in every section the live slots come first. One section has all 32 slots live; each other section has between 16 and 32 live slots, and all sections together have 3 * 32. Over the live slots taken section by section in order, layer ids never fall and every layer has exactly 12 live slots; dead slots hold arbitrary layer ids.
All inputs are finite; a program needn't handle non-finite values.
Results may differ from a plain program's by a relative error of at most 0.008.
Values may be sent and summed in bfloat16 or wider, within the bound.
No kernel may reach another device: no remote copies, remote signals or barrier semaphores. Data moves between devices by JAX's collectives and lax.ppermute only.
A program may use at most 64 MiB of HBM per device.

v0:
```python
import jax
import jax.numpy as jnp
from jax import lax
from jax.sharding import PartitionSpec as P

bias_first = 1.0 - 0.9**10
bias_second = 1.0 - 0.99**10


def carried_in(part, axis, combine, identity):
    place = lax.axis_index(axis)
    gathered = lax.all_gather(part, axis)
    state = jnp.zeros_like(part) + jnp.asarray(identity, part.dtype)

    def one(step, state):
        return combine(state, lax.dynamic_index_in_dim(gathered, step, 0, False))

    return lax.fori_loop(0, place, one, state)


def from_root(block, axis, source):
    block = jnp.where(lax.axis_index(axis) == source, block, jnp.zeros_like(block))
    return lax.psum(block, axis)


def combine_sum(earlier, later):
    return earlier + later


def shards(grad_parts, params, moment_first, moment_second, block_layer, block_valid, decay):
    row_count = params.shape[1]
    local_grad = grad_parts[0, 0]
    gradient = lax.psum_scatter(
        local_grad.astype(jnp.float32).astype(jnp.bfloat16),
        "shard",
        scatter_dimension=0,
        tiled=True,
    ).astype(jnp.float32)
    block_rows = row_count // block_layer.shape[1]
    layer_rows = jnp.repeat(block_layer[0], block_rows)
    valid_rows = jnp.repeat(block_valid[0], block_rows) > 0
    layer_ids = jnp.arange(decay.shape[0], dtype=jnp.int32)
    onehot = jnp.where(
        valid_rows[:, None] & (layer_rows[:, None] == layer_ids[None, :]), 1.0, 0.0
    ).astype(jnp.float32)
    weights = params[0].astype(jnp.float32)
    first = 0.9 * moment_first[0] + 0.1 * gradient
    second = 0.99 * moment_second[0] + 0.01 * gradient * gradient
    row_decay = jnp.dot(onehot, decay, precision=lax.Precision.HIGHEST)
    update = (
        first / bias_first / (jnp.sqrt(second / bias_second) + 1e-06) + row_decay[:, None] * weights
    )
    row_sums = jnp.stack(
        [jnp.sum(weights * weights, axis=-1), jnp.sum(update * update, axis=-1)], axis=1
    )
    partial_value = jnp.dot(onehot.T, row_sums, precision=lax.Precision.HIGHEST)
    section_total = lax.psum(partial_value, "shard")
    before = carried_in(section_total, "section", combine_sum, jnp.zeros_like(section_total))
    through = before + section_total
    totals = from_root(through, "section", lax.axis_size("section") - 1)
    ratios = jnp.sqrt(totals[:, 0] / (totals[:, 1] + 1.0))
    row_ratio = jnp.dot(onehot, ratios, precision=lax.Precision.HIGHEST)
    stepped = weights - 0.1 * row_ratio[:, None] * update
    live = valid_rows[:, None]
    new_params = jnp.where(live, stepped, weights).astype(jnp.bfloat16)
    new_first = jnp.where(live, first, moment_first[0])
    new_second = jnp.where(live, second, moment_second[0])
    return (new_params[None], new_first[None], new_second[None], ratios)


def solution(mesh):
    placed = (
        P("section", "shard", None, None),
        P("section", "shard", None),
        P("section", "shard", None),
        P("section", "shard", None),
        P("section", "shard"),
        P("section", "shard"),
        P(),
    )
    return jax.shard_map(
        shards,
        mesh=mesh,
        in_specs=placed,
        out_specs=(
            P("section", "shard", None),
            P("section", "shard", None),
            P("section", "shard", None),
            P(),
        ),
        check_vma=False,
    )
```

profile of v0, /device:TPU:0, one launch (start us, length us, event | category | flops | bytes accessed | tf_op | source)
XLA Modules:
  0.0 109.7 jit_solution(5550758126043738490)
XLA Ops:
  7.2 0.0 copy-start
  7.2 0.0 copy-start.4
  7.2 0.0 copy-start.3
  7.2 0.0 copy-start.1
  7.2 0.0 copy-start.2
  7.2 0.0 reduce-scatter.2.cloned.1.call-start
  7.3 0.7 reduce-scatter.2.cloned.1.call-update
  8.0 0.0 copy-done.4
  8.0 0.1 broadcast_in_dim.42
  8.1 0.1 gt.20
  8.1 0.0 copy-done.3
  8.1 0.1 broadcast_in_dim.44
  8.2 0.1 eq.18
  8.3 0.0 copy-done
  8.3 0.2 convolution_bitcast_fusion.1
  8.5 56.8 %reduce-scatter.2.cloned.1.call-done = bf16[32,8192]{1,0:T(8,128)(2,1)} async-done(((bf16[256,8192]{1,0:T(8,128)(2,1)}), bf16[32,8192]{1,0:T(8,128)(2,1)}) %reduce-scatter.2.cloned.1.call-update) | async-done | bytes 524304 | tf_op jit(solution)/shard_map/reduce_scatter | solution.py:33
  65.3 0.0 copy-done.1
  65.3 0.0 copy-done.2
  65.3 3.8 %multiply_reduce_fusion = (f32[32]{0:T(128)S(1)}, f32[32,8192]{1,0:T(8,128)S(1)}, f32[1,32,8192]{2,1,0:T(8,128)}, f32[1,32,8192]{2,1,0:T(8,128)}, f32[32]{0:T(128)S(1)}) fusion(bf16[1,32,8192]{2,1,0:T(8,128)(2,1)S(1)} %copy-done.1, f32[32]{0:T(128)S(1)} %convolution_bitcast_fusion.1, f32[1,32,8192]{2,1,0:T(8,128)S(1)} %copy-done.2, ...), kind=kLoop, calls=%fused_computation.26 | loop fusion | flops 5504960 | bytes 6291872 | tf_op jit(solution)/shard_map/reduce_sum | solution.py:54
  69.1 0.2 fusion.15
  69.3 12.5 %psum.14 = f32[8,2]{0,1:T(2,128)S(1)} all-reduce(f32[8,2]{0,1:T(2,128)S(1)} %fusion.15), channel_id=1, replica_groups=mesh['section'=4,'shard'=8] {'shard'}, use_global_device_ids=true, to_apply=%region_3.4 | all-reduce | flops 16 | bytes 128 | tf_op jit(solution)/shard_map/psum | solution.py:57
  81.8 10.9 %all-gather.1 = f32[4,8,2]{1,2,0:T(2,128)S(1)} all-gather(f32[1,8,2]{1,2,0:T(2,128)S(1)} %bitcast.70), channel_id=2, replica_groups=mesh['section'=4,'shard'=8] {'section'}, dimensions={0}, use_global_device_ids=true | all-gather | bytes 320 | tf_op jit(solution)/shard_map/all_gather | solution.py:12
  92.7 8.4 %psum.15 = f32[8,2]{0,1:T(2,128)S(1)} all-reduce(f32[8,2]{0,1:T(2,128)S(1)} %add_select_fusion), channel_id=1, replica_groups=mesh['section'=4,'shard'=8] {'section'}, use_global_device_ids=true, to_apply=%region_6.7 | all-reduce | flops 16 | bytes 128 | tf_op jit(solution)/shard_map/psum | solution.py:23
  101.1 0.2 fusion
  101.3 0.5 fusion.48
  101.8 1.0 fusion.13
  (4 shorter events, 0.0 us)
Async XLA Ops:
  7.2 1.1 %copy-start = (f32[8]{0:T(128)S(1)}, f32[8]{0:T(128)}, u32[]{:S(2)}) copy-start(f32[8]{0:T(128)} %param.15) | copy-start | bytes 100
  7.2 0.8 copy-start.4
  7.2 1.0 copy-start.3
  7.2 58.1 %copy-start.1 = (bf16[1,32,8192]{2,1,0:T(8,128)(2,1)S(1)}, bf16[1,32,8192]{2,1,0:T(8,128)(2,1)}, u32[]{:S(2)}) copy-start(bf16[1,32,8192]{2,1,0:T(8,128)(2,1)} %param.10) | copy-start | bytes 1572868
  7.2 58.1 %copy-start.2 = (f32[1,32,8192]{2,1,0:T(8,128)S(1)}, f32[1,32,8192]{2,1,0:T(8,128)}, u32[]{:S(2)}) copy-start(f32[1,32,8192]{2,1,0:T(8,128)} %param.12) | copy-start | bytes 3145732
  7.2 58.1 %reduce-scatter.2.cloned.1.call-start = ((), (), s32[]{:S(2)}) async-start(), calls=%async_computation.1 | async-start | bytes 4718592 | tf_op jit(solution)/shard_map/reduce_scatter | solution.py:33
Sparse Core Ops, SparseCore 0:
  11.4 53.8 reduce-scatter.1
where the time goes:
time: 110 us
  waiting for transfers between devices  57.5 us (52%)
  blocking collectives  31.8 us (29%)
  between operations  14.1 us (13%)
  other arithmetic  5.4 us (5%)
    reduce_scatter x1, waiting for transfers between devices, shards(): lax.psum_scatter(local_grad.astype(jnp.float32).astype(jnp.bfloat16), 'sh...  56.8 us
    psum x1, blocking collectives, shards(): section_total = lax.psum(partial_value, 'shard')  12.5 us
    all_gather x1, blocking collectives, carried_in(): gathered = lax.all_gather(part, axis)  10.9 us
    psum x1, blocking collectives, from_root(): return lax.psum(block, axis)  8.37 us
    reduce_sum x1, other arithmetic, shards(): jnp.sum(update * update, axis=-1)  3.8 us
  transfers between devices with their start and end apart: 1, of which 1 were waited for; matrix products, arithmetic and copies ran while one was open for 0% of the time, Pallas kernels for 0%

commit v1 on v0

--- a/solution.py
+++ b/solution.py
@@ -54,7 +54,8 @@
         [jnp.sum(weights * weights, axis=-1), jnp.sum(update * update, axis=-1)], axis=1
     )
     partial_value = jnp.dot(onehot.T, row_sums, precision=lax.Precision.HIGHEST)
-    section_total = lax.psum(partial_value, "shard")
+    parts = lax.all_gather(partial_value, "shard")
+    section_total = jnp.sum(parts, axis=0)
     before = carried_in(section_total, "section", combine_sum, jnp.zeros_like(section_total))
     through = before + section_total
     totals = from_root(through, "section", lax.axis_size("section") - 1)

time: 110 us -> 106 us (0.964)
  blocking collectives: 31.8 us -> 28.1 us
    psum x1 -> x0, blocking collectives: 12.5 us -> none  [shards(): section_total = lax.psum(partial_value, 'shard')]
    all_gather x0 -> x1, blocking collectives: none -> 8.87 us  [shards(): parts = lax.all_gather(partial_value, 'shard')]
where the time goes in v1:
time: 106 us
  waiting for transfers between devices  57.5 us (54%)
  blocking collectives  28.1 us (27%)
  between operations  14.1 us (13%)
  other arithmetic  5.42 us (5%)
    reduce_scatter x1, waiting for transfers between devices, shards(): lax.psum_scatter(local_grad.astype(jnp.float32).astype(jnp.bfloat16), 'sh...  56.8 us
    all_gather x1, blocking collectives, carried_in(): gathered = lax.all_gather(part, axis)  10.9 us
    all_gather x1, blocking collectives, shards(): parts = lax.all_gather(partial_value, 'shard')  8.87 us
    psum x1, blocking collectives, from_root(): return lax.psum(block, axis)  8.37 us
    reduce_sum x1, other arithmetic, shards(): jnp.sum(update * update, axis=-1)  3.8 us
  transfers between devices with their start and end apart: 1, of which 1 were waited for; matrix products, arithmetic and copies ran while one was open for 0% of the time, Pallas kernels for 0%

profile of v1, /device:TPU:0, one launch (start us, length us, event | category | flops | bytes accessed | tf_op | source)
XLA Modules:
  0.0 106.1 jit_solution(11892992813210922322)
XLA Ops:
  7.2 0.0 copy-start
  7.2 0.0 copy-start.4
  7.2 0.0 copy-start.3
  7.2 0.0 copy-start.1
  7.2 0.0 copy-start.2
  7.2 0.0 reduce-scatter.2.cloned.1.call-start
  7.3 0.7 reduce-scatter.2.cloned.1.call-update
  8.0 0.0 copy-done.4
  8.0 0.1 broadcast_in_dim.42
  8.1 0.1 gt.20
  8.1 0.0 copy-done.3
  8.2 0.1 broadcast_in_dim.44
  8.2 0.1 eq.18
  8.3 0.0 copy-done
  8.3 0.2 convolution_bitcast_fusion.2
  8.5 56.8 %reduce-scatter.2.cloned.1.call-done = bf16[32,8192]{1,0:T(8,128)(2,1)} async-done(((bf16[256,8192]{1,0:T(8,128)(2,1)}), bf16[32,8192]{1,0:T(8,128)(2,1)}) %reduce-scatter.2.cloned.1.call-update) | async-done | bytes 524304 | tf_op jit(solution)/shard_map/reduce_scatter | solution.py:33
  65.3 0.0 copy-done.1
  65.3 0.0 copy-done.2
  65.3 3.8 %multiply_reduce_fusion = (f32[32]{0:T(128)S(1)}, f32[32,8192]{1,0:T(8,128)S(1)}, f32[1,32,8192]{2,1,0:T(8,128)}, f32[1,32,8192]{2,1,0:T(8,128)}, f32[32]{0:T(128)S(1)}) fusion(bf16[1,32,8192]{2,1,0:T(8,128)(2,1)S(1)} %copy-done.1, f32[32]{0:T(128)S(1)} %convolution_bitcast_fusion.2, f32[1,32,8192]{2,1,0:T(8,128)S(1)} %copy-done.2, ...), kind=kLoop, calls=%fused_computation.27 | loop fusion | flops 5504960 | bytes 6291872 | tf_op jit(solution)/shard_map/reduce_sum | solution.py:54
  69.1 0.2 convolution_bitcast_fusion
  69.3 8.9 %all-gather.2 = f32[8,8,2]{1,2,0:T(2,128)S(1)} all-gather(f32[1,8,2]{1,2,0:T(2,128)S(1)} %convolution_bitcast_fusion), channel_id=2, replica_groups=mesh['section'=4,'shard'=8] {'shard'}, dimensions={0}, use_global_device_ids=true | all-gather | bytes 576 | tf_op jit(solution)/shard_map/all_gather | solution.py:57
  78.2 10.9 %all-gather.3 = f32[4,8,2]{1,2,0:T(2,128)S(1)} all-gather(f32[1,8,2]{1,2,0:T(2,128)S(1)} %bitcast.72), channel_id=3, replica_groups=mesh['section'=4,'shard'=8] {'section'}, dimensions={0}, use_global_device_ids=true | all-gather | bytes 320 | tf_op jit(solution)/shard_map/all_gather | solution.py:12
  89.1 8.4 %psum.7 = f32[8,2]{0,1:T(2,128)S(1)} all-reduce(f32[8,2]{0,1:T(2,128)S(1)} %add_select_fusion), channel_id=1, replica_groups=mesh['section'=4,'shard'=8] {'section'}, use_global_device_ids=true, to_apply=%region_6.7 | all-reduce | flops 16 | bytes 128 | tf_op jit(solution)/shard_map/psum | solution.py:23
  97.5 0.2 fusion
  97.7 0.5 fusion.47
  98.2 1.0 fusion.13
  (5 shorter events, 0.0 us)
Async XLA Ops:
  7.2 1.1 %copy-start = (f32[8]{0:T(128)S(1)}, f32[8]{0:T(128)}, u32[]{:S(2)}) copy-start(f32[8]{0:T(128)} %param.15) | copy-start | bytes 100
  7.2 0.8 copy-start.4
  7.2 1.0 copy-start.3
  7.2 58.1 %copy-start.1 = (bf16[1,32,8192]{2,1,0:T(8,128)(2,1)S(1)}, bf16[1,32,8192]{2,1,0:T(8,128)(2,1)}, u32[]{:S(2)}) copy-start(bf16[1,32,8192]{2,1,0:T(8,128)(2,1)} %param.10) | copy-start | bytes 1572868
  7.2 58.1 %copy-start.2 = (f32[1,32,8192]{2,1,0:T(8,128)S(1)}, f32[1,32,8192]{2,1,0:T(8,128)}, u32[]{:S(2)}) copy-start(f32[1,32,8192]{2,1,0:T(8,128)} %param.12) | copy-start | bytes 3145732
  7.2 58.1 %reduce-scatter.2.cloned.1.call-start = ((), (), s32[]{:S(2)}) async-start(), calls=%async_computation.1 | async-start | bytes 4718592 | tf_op jit(solution)/shard_map/reduce_scatter | solution.py:33
Sparse Core Ops, SparseCore 0:
  11.4 53.8 reduce-scatter.1
